TPU v7x, 128 devices: a whole 4x4x4 slice. The times are simulated.
128 devices in a mesh: row: 8 (over z, x_hi), col: 16 (over y, x_lo, core).
Axes of the slice: x: 4 (x_hi: 2, x_lo: 2; x = x_hi * 2 + x_lo), y: 4, z: 4, core: 2. Of those that a mesh axis runs over, the one named last changes fastest.
Arguments:
- node_feats: bfloat16 [16384, 512], P(('row', 'col')), may hold values from -80 to 80
- block_mask: int32 [128, 128], replicated, may hold values from 0 to 1, as said below
- w_qkv: bfloat16 [2, 512, 1536], replicated, may hold values from -0.25 to 0.25
- w_out: bfloat16 [2, 512, 512], replicated, may hold values from -0.79296875 to 0.79296875
- w_up: bfloat16 [2, 512, 1024], replicated, may hold values from -0.25 to 0.25
- w_down: bfloat16 [2, 1024, 512], replicated, may hold values from -0.1875 to 0.1875
- ln_gain: float32 [2, 2, 512], replicated, may hold values from 0.1 to 1.9
- ln_bias: float32 [2, 2, 512], replicated, may hold values from -3 to 3
Outputs:
- nodes_out: bfloat16 [16384, 512], P(('row', 'col'))
Inputs may be any that keep to these rules, and one draw needn't show every extreme that they name: `block_mask`: A symmetric 0/1 table over the 128 node blocks; every block is linked with itself.
All inputs are finite; a program needn't handle non-finite values.
Results may differ from a plain program's by a relative error of at most 0.022.
Values may be sent and summed in bfloat16 or wider, within the bound.
A program may use at most 128 MiB of HBM per device.

v0:
```python
import jax
import jax.numpy as jnp
from jax import lax
from jax.sharding import PartitionSpec as P

HEADS = 8
BLOCK = 128
LAYERS = 2


def copy_for_each(x, axis):
    length = lax.axis_size(axis)
    return lax.all_to_all(jnp.broadcast_to(x[None], (length, *x.shape)), axis, 0, 0, tiled=True)


def joined_along(tiles, dim):
    lengths = list(tiles.shape[1:])
    lengths[dim] *= tiles.shape[0]
    return jnp.moveaxis(tiles, 0, dim).reshape(lengths)


def gathered_copies(x, axis, dim):
    tiles = copy_for_each(x, axis)
    return joined_along(tiles, dim)


def over_copies(x, axis):
    return copy_for_each(x, axis).max(axis=0)


def split_up(x, dim, length):
    lengths = x.shape
    tiles = x.reshape(*lengths[:dim], length, lengths[dim] // length, *lengths[dim + 1 :])
    return jnp.moveaxis(tiles, dim, 0)


def sent_and_summed(x, axis, dim):
    tiles = split_up(x, dim, lax.axis_size(axis))
    arrived = lax.all_to_all(tiles, axis, split_axis=0, concat_axis=0, tiled=True)
    return arrived.astype(jnp.float32).sum(axis=0)


def side_by_side(arrays, axis, dim, along):
    both = jnp.concatenate(arrays, axis=along)
    whole, at, outs = (sent_and_summed(both, axis, dim), 0, [])
    for a in arrays:
        outs.append(lax.slice_in_dim(whole, at, at + a.shape[along], axis=along))
        at += a.shape[along]
    return tuple(outs)


def layer_norm(values, gain, bias):
    center = values - jnp.mean(values, axis=-1, keepdims=True)
    spread = jnp.mean(center * center, axis=-1, keepdims=True)
    return center * lax.rsqrt(spread + 1e-05) * gain + bias


def per_head(summed, factor):
    count = summed.shape[0]
    return (summed.reshape(count, factor.shape[1], -1) * factor[:, :, None]).reshape(summed.shape)


def partial_attention(queries, keys, values, sub_mask, heads):
    qrows, width = queries.shape
    head_dim = width // heads
    qblock = min(512, qrows)
    nblocks = qrows // qblock
    qsplit = queries.reshape(nblocks, qblock, heads, head_dim)
    ksplit = keys.reshape(-1, heads, head_dim)
    vsplit = values.reshape(-1, heads, head_dim)
    mask_rows = sub_mask.reshape(nblocks, qblock // BLOCK, -1)

    def one_block(item):
        qpart, mpart = item
        scores = jnp.einsum("qhd,khd->hqk", qpart, ksplit, preferred_element_type=jnp.float32) * (
            1.0 / head_dim**0.5
        )
        allowed = (jnp.repeat(jnp.repeat(mpart, BLOCK, axis=0), BLOCK, axis=1) > 0)[None]
        peak = jnp.max(jnp.where(allowed, scores, -1e30), axis=-1, keepdims=True)
        weights = jnp.where(allowed, jnp.exp(scores - peak), 0.0)
        mass = jnp.sum(weights, axis=-1)
        summed = jnp.einsum(
            "hqk,khd->qhd", weights.astype(jnp.bfloat16), vsplit, preferred_element_type=jnp.float32
        )
        return (summed.reshape(qblock, width), peak[:, :, 0].T, mass.T)

    summed, peak, mass = lax.map(one_block, (qsplit, mask_rows))
    return (summed.reshape(qrows, width), peak.reshape(qrows, heads), mass.reshape(qrows, heads))


def per_device(node_feats, block_mask, w_qkv, w_out, w_up, w_down, ln_gain, ln_bias):
    rows, width = node_feats.shape
    heads = HEADS
    n_col = lax.axis_size("col")
    n_row = lax.axis_size("row")
    row_index = lax.axis_index("row")
    col_index = lax.axis_index("col")
    blk_dev = rows // BLOCK
    group_ids = row_index * (n_col * blk_dev) + jnp.arange(n_col * blk_dev, dtype=jnp.int32)
    column_ids = (
        (jnp.arange(n_row, dtype=jnp.int32)[:, None] * n_col + col_index) * blk_dev
        + jnp.arange(blk_dev, dtype=jnp.int32)[None, :]
    ).reshape(-1)
    query_ids, key_ids, own_start = (column_ids, group_ids, row_index * rows)
    sub_mask = jnp.take(jnp.take(block_mask, query_ids, axis=0), key_ids, axis=1)
    x = node_feats
    for layer in range(LAYERS):
        weights = w_qkv[layer]
        own_q = jnp.dot(x, weights[:, :width], preferred_element_type=jnp.float32).astype(
            jnp.bfloat16
        )
        gathered = lax.all_gather(x, "col", axis=0, tiled=True)
        kv_both = jnp.dot(gathered, weights[:, width:], preferred_element_type=jnp.float32).astype(
            jnp.bfloat16
        )
        keys = kv_both[:, :width]
        values = kv_both[:, width:]
        queries = gathered_copies(own_q, "row", 0)
        summed, peak, mass = partial_attention(queries, keys, values, sub_mask, heads)
        top = over_copies(peak.astype(jnp.bfloat16), "row").astype(peak.dtype)
        factor = jnp.exp(peak - top)
        summed, mass = side_by_side(
            (per_head(summed, factor).astype(jnp.bfloat16), (mass * factor).astype(jnp.bfloat16)),
            "row",
            0,
            1,
        )
        attn = per_head(summed, 1.0 / mass).astype(jnp.bfloat16)
        mixed = jnp.dot(attn, w_out[layer], preferred_element_type=jnp.float32)
        hidden = layer_norm(
            x.astype(jnp.float32) + mixed, ln_gain[layer, 0], ln_bias[layer, 0]
        ).astype(jnp.bfloat16)
        up = jax.nn.gelu(jnp.dot(hidden, w_up[layer], preferred_element_type=jnp.float32)).astype(
            jnp.bfloat16
        )
        down = jnp.dot(up, w_down[layer], preferred_element_type=jnp.float32)
        x = layer_norm(
            hidden.astype(jnp.float32) + down, ln_gain[layer, 1], ln_bias[layer, 1]
        ).astype(jnp.bfloat16)
    return x


def solution(mesh):
    placed = (P(("row", "col"), None), P(), P(), P(), P(), P(), P(), P())
    return jax.shard_map(
        per_device, mesh=mesh, in_specs=placed, out_specs=P(("row", "col"), None), check_vma=False
    )
```

profile of v0, /device:TPU:1, one launch (start us, length us, event | category | flops | bytes accessed | tf_op | source)
XLA Modules:
  0.0 400.1 jit_solution(2491265612144790777)
XLA Ops:
  13.1 8.3 %all-to-all-start = ((bf16[8,128,512]{1,2,0:T(8,128)(2,1)}), bf16[8,128,512]{1,2,0:T(8,128)(2,1)S(1)}, u32[]{:S(2)}, u32[]{:S(2)}) async-start(bf16[8,128,512]{1,2,0:T(8,128)(2,1)} %broadcast_in_dim.129), calls=%async_computation | async-start | bytes 2097152 | tf_op jit(solution)/shard_map/all_to_all | solution.py:13
  22.9 24.1 %all-to-all-done = bf16[8,128,512]{1,2,0:T(8,128)(2,1)S(1)} async-done(((bf16[8,128,512]{1,2,0:T(8,128)(2,1)}), bf16[8,128,512]{1,2,0:T(8,128)(2,1)S(1)}, u32[]{:S(2)}, u32[]{:S(2)}) %all-to-all-start) | async-done | bytes 1048608 | tf_op jit(solution)/shard_map/all_to_all | solution.py:13
  50.0 4.0 convolution_convert_fusion.1
  57.3 102.6 %while.28 = (s32[]{:T(128)}, f32[2,512,512]{2,1,0:T(8,128)}, f32[2,512,8]{1,2,0:T(8,128)S(1)}, f32[2,512,8]{1,2,0:T(8,128)S(1)}, s32[2,4,16]{2,1,0:T(4,128)S(1)}...) while((s32[]{:T(128)}, f32[2,512,512]{2,1,0:T(8,128)}, ...), condition=%wide.region_3.4_spmd, body=%wide.region_0.3_spmd.sunk | while | flops 2239750144 | bytes 121259008 | solution.py:87
  61.5 13.8 %select_reduce_fusion.4 = (f32[8,512]{1,0:T(8,128)S(1)}, f32[8,512,2048]{2,1,0:T(8,128)}) fusion(pred[512,2048]{1,0:T(8,128)(4,1)S(1)} %bitcast.198, bf16[2048,8,64]{0,2,1:T(8,128)(2,1)S(1)} %get-tuple-element.347, bf16[2,512,8,64]{1,3,2,0:T(8,128)(2,1)S(1)} %copy-done.3, s32[]{:T(128)} %get-tuple-element.332), kind=kOutput, calls=%fused_computation.3.clone.1 | convolution fusion | flops 1098903552 | bytes 37240836 | tf_op jit(solution)/shard_map/while/body/eval_jaxpr/qhd,khd->hqk/dot_general | solution.py:75
  75.4 15.2 %fusion.151 = f32[8,512]{1,0:T(8,128)S(1)} fusion(f32[8,512,2048]{2,1,0:T(8,128)} %get-tuple-element.307, f32[8,512]{1,0:T(8,128)S(1)} %get-tuple-element.308, pred[512,2048]{1,0:T(8,128)(4,1)S(1)} %bitcast.199), kind=kLoop, calls=%fused_computation.4.clone.1 | loop fusion | flops 33550336 | bytes 34635776 | tf_op jit(solution)/shard_map/while/body/eval_jaxpr/reduce_sum | solution.py:81
  90.5 15.5 %fusion.150 = f32[8,512,64]{1,2,0:T(8,128)} fusion(bf16[2048,8,64]{0,2,1:T(8,128)(2,1)} %get-tuple-element.348, f32[8,512,2048]{2,1,0:T(8,128)} %get-tuple-element.307, f32[8,512]{1,0:T(8,128)S(1)} %get-tuple-element.308, pred[512,2048]{1,0:T(8,128)(4,1)S(1)} %bitcast.200), kind=kOutput, calls=%fused_computation.6.clone.1 | convolution fusion | flops 1107296256 | bytes 37765120 | tf_op jit(solution)/shard_map/while/body/eval_jaxpr/hqk,khd->qhd/dot_general | solution.py:82
  112.8 13.8 %select_reduce_fusion.4 = (f32[8,512]{1,0:T(8,128)S(1)}, f32[8,512,2048]{2,1,0:T(8,128)}) fusion(pred[512,2048]{1,0:T(8,128)(4,1)S(1)} %bitcast.198, bf16[2048,8,64]{0,2,1:T(8,128)(2,1)S(1)} %get-tuple-element.347, bf16[2,512,8,64]{1,3,2,0:T(8,128)(2,1)S(1)} %copy-done.3, s32[]{:T(128)} %get-tuple-element.332), kind=kOutput, calls=%fused_computation.3.clone.1 | convolution fusion | flops 1098903552 | bytes 37240836 | tf_op jit(solution)/shard_map/while/body/eval_jaxpr/qhd,khd->hqk/dot_general | solution.py:75
  126.6 15.2 %fusion.151 = f32[8,512]{1,0:T(8,128)S(1)} fusion(f32[8,512,2048]{2,1,0:T(8,128)} %get-tuple-element.307, f32[8,512]{1,0:T(8,128)S(1)} %get-tuple-element.308, pred[512,2048]{1,0:T(8,128)(4,1)S(1)} %bitcast.199), kind=kLoop, calls=%fused_computation.4.clone.1 | loop fusion | flops 33550336 | bytes 34635776 | tf_op jit(solution)/shard_map/while/body/eval_jaxpr/reduce_sum | solution.py:81
  141.8 15.5 %fusion.150 = f32[8,512,64]{1,2,0:T(8,128)} fusion(bf16[2048,8,64]{0,2,1:T(8,128)(2,1)} %get-tuple-element.348, f32[8,512,2048]{2,1,0:T(8,128)} %get-tuple-element.307, f32[8,512]{1,0:T(8,128)S(1)} %get-tuple-element.308, pred[512,2048]{1,0:T(8,128)(4,1)S(1)} %bitcast.200), kind=kOutput, calls=%fused_computation.6.clone.1 | convolution fusion | flops 1107296256 | bytes 37765120 | tf_op jit(solution)/shard_map/while/body/eval_jaxpr/hqk,khd->qhd/dot_general | solution.py:82
  160.0 11.3 %all_to_all.30 = bf16[8,1024,8]{1,2,0:T(8,128)(2,1)S(1)} all-to-all(bf16[8,1024,8]{1,2,0:T(8,128)(2,1)S(1)} %broadcast_in_dim.130), channel_id=1, replica_groups=mesh['row'=8,'col'=16] {'row'}, dimensions={0} | all-to-all | bytes 262144 | tf_op jit(solution)/shard_map/all_to_all | solution.py:13
  185.3 13.9 %all-to-all-done.2 = bf16[8,128,520]{1,2,0:T(8,128)(2,1)S(1)} async-done(((bf16[8,128,520]{1,2,0:T(8,128)(2,1)}), bf16[8,128,520]{1,2,0:T(8,128)(2,1)S(1)}, u32[]{:S(2)}, u32[]{:S(2)}) %all-to-all-start.2) | async-done | bytes 1064992 | tf_op jit(solution)/shard_map/all_to_all | solution.py:39
  205.1 25.8 %all_to_all.31 = bf16[8,128,512]{1,2,0:T(8,128)(2,1)S(1)} all-to-all(bf16[8,128,512]{1,2,0:T(8,128)(2,1)S(1)} %broadcast_in_dim.131), channel_id=1, replica_groups=mesh['row'=8,'col'=16] {'row'}, dimensions={0} | all-to-all | bytes 2097152 | tf_op jit(solution)/shard_map/all_to_all | solution.py:13
  233.2 4.8 %all-gather.5.cloned.1.call-done = bf16[2048,512]{1,0:T(8,128)(2,1)} async-done(((bf16[128,512]{1,0:T(8,128)(2,1)}), bf16[2048,512]{1,0:T(8,128)(2,1)}) %all-gather.5.cloned.1.call-update) | async-done | bytes 2097168 | tf_op jit(solution)/shard_map/all_gather | solution.py:112
  238.0 4.2 %convolution_convert_fusion = bf16[2048,1024]{0,1:T(8,128)(2,1)S(1)} fusion(bf16[2048,512]{1,0:T(8,128)(2,1)} %all-gather.5.cloned.1.call-done, bf16[512,1536]{1,0:T(8,128)(2,1)} %get-tuple-element.191), kind=kOutput, calls=%fused_computation.38 | convolution fusion | flops 2149580800 | bytes 7340032 | tf_op jit(solution)/shard_map/dot_general | solution.py:113
  245.6 102.7 %while.29 = (s32[]{:T(128)}, f32[2,512,512]{2,1,0:T(8,128)}, f32[2,512,8]{1,2,0:T(8,128)S(1)}, f32[2,512,8]{1,2,0:T(8,128)S(1)}, s32[2,4,16]{2,1,0:T(4,128)S(1)}...) while((s32[]{:T(128)}, f32[2,512,512]{2,1,0:T(8,128)}, ...), condition=%wide.region_13.14_spmd, body=%wide.region_10.13_spmd.sunk | while | flops 2239750144 | bytes 121259008 | solution.py:87
  249.8 13.8 %select_reduce_fusion.5 = (f32[8,512]{1,0:T(8,128)S(1)}, f32[8,512,2048]{2,1,0:T(8,128)}) fusion(pred[512,2048]{1,0:T(8,128)(4,1)S(1)} %bitcast.201, bf16[2048,8,64]{0,2,1:T(8,128)(2,1)S(1)} %get-tuple-element.374, bf16[2,512,8,64]{1,3,2,0:T(8,128)(2,1)S(1)} %copy-done.2, s32[]{:T(128)} %get-tuple-element.359), kind=kOutput, calls=%fused_computation.21.clone.1 | convolution fusion | flops 1098903552 | bytes 37240836 | tf_op jit(solution)/shard_map/while/body/eval_jaxpr/qhd,khd->hqk/dot_general | solution.py:75
  263.6 15.2 %fusion.157 = f32[8,512]{1,0:T(8,128)S(1)} fusion(f32[8,512,2048]{2,1,0:T(8,128)} %get-tuple-element.319, f32[8,512]{1,0:T(8,128)S(1)} %get-tuple-element.320, pred[512,2048]{1,0:T(8,128)(4,1)S(1)} %bitcast.202), kind=kLoop, calls=%fused_computation.22.clone.1 | loop fusion | flops 33550336 | bytes 34635776 | tf_op jit(solution)/shard_map/while/body/eval_jaxpr/reduce_sum | solution.py:81
  278.8 15.5 %fusion.156 = f32[8,512,64]{1,2,0:T(8,128)} fusion(bf16[2048,8,64]{0,2,1:T(8,128)(2,1)} %get-tuple-element.375, f32[8,512,2048]{2,1,0:T(8,128)} %get-tuple-element.319, f32[8,512]{1,0:T(8,128)S(1)} %get-tuple-element.320, pred[512,2048]{1,0:T(8,128)(4,1)S(1)} %bitcast.203), kind=kOutput, calls=%fused_computation.24.clone.1 | convolution fusion | flops 1107296256 | bytes 37765120 | tf_op jit(solution)/shard_map/while/body/eval_jaxpr/hqk,khd->qhd/dot_general | solution.py:82
  301.1 13.8 %select_reduce_fusion.5 = (f32[8,512]{1,0:T(8,128)S(1)}, f32[8,512,2048]{2,1,0:T(8,128)}) fusion(pred[512,2048]{1,0:T(8,128)(4,1)S(1)} %bitcast.201, bf16[2048,8,64]{0,2,1:T(8,128)(2,1)S(1)} %get-tuple-element.374, bf16[2,512,8,64]{1,3,2,0:T(8,128)(2,1)S(1)} %copy-done.2, s32[]{:T(128)} %get-tuple-element.359), kind=kOutput, calls=%fused_computation.21.clone.1 | convolution fusion | flops 1098903552 | bytes 37240836 | tf_op jit(solution)/shard_map/while/body/eval_jaxpr/qhd,khd->hqk/dot_general | solution.py:75
  314.9 15.2 %fusion.157 = f32[8,512]{1,0:T(8,128)S(1)} fusion(f32[8,512,2048]{2,1,0:T(8,128)} %get-tuple-element.319, f32[8,512]{1,0:T(8,128)S(1)} %get-tuple-element.320, pred[512,2048]{1,0:T(8,128)(4,1)S(1)} %bitcast.202), kind=kLoop, calls=%fused_computation.22.clone.1 | loop fusion | flops 33550336 | bytes 34635776 | tf_op jit(solution)/shard_map/while/body/eval_jaxpr/reduce_sum | solution.py:81
  330.1 15.5 %fusion.156 = f32[8,512,64]{1,2,0:T(8,128)} fusion(bf16[2048,8,64]{0,2,1:T(8,128)(2,1)} %get-tuple-element.375, f32[8,512,2048]{2,1,0:T(8,128)} %get-tuple-element.319, f32[8,512]{1,0:T(8,128)S(1)} %get-tuple-element.320, pred[512,2048]{1,0:T(8,128)(4,1)S(1)} %bitcast.203), kind=kOutput, calls=%fused_computation.24.clone.1 | convolution fusion | flops 1107296256 | bytes 37765120 | tf_op jit(solution)/shard_map/while/body/eval_jaxpr/hqk,khd->qhd/dot_general | solution.py:82
  348.3 13.1 %all_to_all.32 = bf16[8,1024,8]{1,2,0:T(8,128)(2,1)S(1)} all-to-all(bf16[8,1024,8]{1,2,0:T(8,128)(2,1)S(1)} %broadcast_in_dim.132), channel_id=1, replica_groups=mesh['row'=8,'col'=16] {'row'}, dimensions={0} | all-to-all | bytes 262144 | tf_op jit(solution)/shard_map/all_to_all | solution.py:13
  369.7 18.4 %all_to_all.33 = bf16[8,128,520]{1,2,0:T(8,128)(2,1)S(1)} all-to-all(bf16[8,128,520]{1,2,0:T(8,128)(2,1)S(1)} %copy.73), channel_id=1, replica_groups=mesh['row'=8,'col'=16] {'row'}, dimensions={0} | all-to-all | bytes 2129920 | tf_op jit(solution)/shard_map/all_to_all | solution.py:39
  (165 shorter events, 80.0 us)
Async XLA Ops:
  6.5 15.0 %copy-start = (s32[128,128]{1,0:T(8,128)S(1)}, s32[128,128]{1,0:T(8,128)}, u32[]{:S(2)}) copy-start(s32[128,128]{1,0:T(8,128)} %param.13) | copy-start | bytes 196612
  6.5 42.9 %all-gather.3.cloned.1.call-start = ((), (), s32[]{:S(2)}) async-start(), calls=%async_computation.6 | async-start | bytes 2228224 | tf_op jit(solution)/shard_map/all_gather | solution.py:112
  7.3 4.4 %copy-start.11 = (bf16[128,512]{1,0:T(8,128)(2,1)S(1)}, bf16[128,512]{1,0:T(8,128)(2,1)}, u32[]{:S(2)}) copy-start(bf16[128,512]{1,0:T(8,128)(2,1)} %param.12) | copy-start | bytes 393220
  10.5 1.1 copy-start.6
  13.1 33.9 %all-to-all-start = ((bf16[8,128,512]{1,2,0:T(8,128)(2,1)}), bf16[8,128,512]{1,2,0:T(8,128)(2,1)S(1)}, u32[]{:S(2)}, u32[]{:S(2)}) async-start(bf16[8,128,512]{1,2,0:T(8,128)(2,1)} %broadcast_in_dim.129), calls=%async_computation | async-start | bytes 2097152 | tf_op jit(solution)/shard_map/all_to_all | solution.py:13
  48.2 1.8 copy-start.7
  57.4 4.2 %copy-start.3 = (bf16[2,512,8,64]{1,3,2,0:T(8,128)(2,1)S(1)}, bf16[2,512,8,64]{1,3,2,0:T(8,128)(2,1)}, u32[]{:S(2)}) copy-start(bf16[2,512,8,64]{1,3,2,0:T(8,128)(2,1)} %get-tuple-element.346) | copy-start | bytes 3145732 | tf_op jit(solution)/shard_map/while
  108.7 4.1 %copy-start.3 = (bf16[2,512,8,64]{1,3,2,0:T(8,128)(2,1)S(1)}, bf16[2,512,8,64]{1,3,2,0:T(8,128)(2,1)}, u32[]{:S(2)}) copy-start(bf16[2,512,8,64]{1,3,2,0:T(8,128)(2,1)} %get-tuple-element.346) | copy-start | bytes 3145732 | tf_op jit(solution)/shard_map/while
  173.3 3.3 copy-start.5
  178.7 5.3 %copy-start.15 = (f32[2,2,512]{2,1,0:T(2,128)S(1)}, f32[2,2,512]{2,1,0:T(2,128)}, u32[]{:S(2)}) copy-start(f32[2,2,512]{2,1,0:T(2,128)} %param.18) | copy-start | bytes 24580
  178.8 5.9 %copy-start.16 = (f32[2,2,512]{2,1,0:T(2,128)S(1)}, f32[2,2,512]{2,1,0:T(2,128)}, u32[]{:S(2)}) copy-start(f32[2,2,512]{2,1,0:T(2,128)} %param.19) | copy-start | bytes 24580
  180.2 19.0 %all-to-all-start.2 = ((bf16[8,128,520]{1,2,0:T(8,128)(2,1)}), bf16[8,128,520]{1,2,0:T(8,128)(2,1)S(1)}, u32[]{:S(2)}, u32[]{:S(2)}) async-start(bf16[8,128,520]{1,2,0:T(8,128)(2,1)} %copy.63), calls=%async_computation.2 | async-start | bytes 2129920 | tf_op jit(solution)/shard_map/all_to_all | solution.py:39
  183.8 15.9 %copy-start.9 = (bf16[2,512,512]{2,1,0:T(8,128)(2,1)S(1)}, bf16[2,512,512]{2,1,0:T(8,128)(2,1)}, u32[]{:S(2)}) copy-start(bf16[2,512,512]{2,1,0:T(8,128)(2,1)} %param.15) | copy-start | bytes 3145732
  183.8 15.9 %copy-start.12 = (bf16[128,512]{1,0:T(8,128)(2,1)S(1)}, bf16[128,512]{1,0:T(8,128)(2,1)}, u32[]{:S(2)}) copy-start(bf16[128,512]{1,0:T(8,128)(2,1)} %param.12) | copy-start | bytes 393220
  183.8 54.2 %all-gather.5.cloned.1.call-start = ((), (), s32[]{:S(2)}) async-start(), calls=%async_computation.7 | async-start | bytes 2228224 | tf_op jit(solution)/shard_map/all_gather | solution.py:112
  245.6 4.2 %copy-start.2 = (bf16[2,512,8,64]{1,3,2,0:T(8,128)(2,1)S(1)}, bf16[2,512,8,64]{1,3,2,0:T(8,128)(2,1)}, u32[]{:S(2)}) copy-start(bf16[2,512,8,64]{1,3,2,0:T(8,128)(2,1)} %get-tuple-element.373) | copy-start | bytes 3145732 | tf_op jit(solution)/shard_map/while
  296.9 4.1 %copy-start.2 = (bf16[2,512,8,64]{1,3,2,0:T(8,128)(2,1)S(1)}, bf16[2,512,8,64]{1,3,2,0:T(8,128)(2,1)}, u32[]{:S(2)}) copy-start(bf16[2,512,8,64]{1,3,2,0:T(8,128)(2,1)} %get-tuple-element.373) | copy-start | bytes 3145732 | tf_op jit(solution)/shard_map/while
  363.5 3.3 copy-start.4
  388.1 1.3 copy-start.10
  388.2 1.7 copy-start.17
  388.2 1.7 copy-start.18
  389.9 3.3 copy-start.1
  389.9 2.5 copy-start.13
  389.9 2.5 copy-start.14
  (1 other events, 0.9 us)
Sparse Core Ops, SparseCore 0:
  9.0 39.0 all-gather.2
  203.6 34.3 all-gather.4
where the time goes:
time: 403 us; the launch traced here: 400 us
  matrix products  132 us (33%)
  blocking collectives  68.6 us (17%)
  other arithmetic  67.7 us (17%)
  local copies, waits for them, and re-layouts  61.7 us (15%)
  waiting for transfers between devices  43.6 us (11%)
  between operations  13.9 us (3%)
  starting transfers between devices  12.1 us (3%)
    dot_general x4, matrix products, one_block(): jnp.einsum('hqk,khd->qhd', weights.astype(jnp.bfloat16), vsplit, preferre...  62 us
    reduce_sum x4, other arithmetic, one_block(): mass = jnp.sum(weights, axis=-1)  60.7 us
    dot_general x4, matrix products, one_block(): jnp.einsum('qhd,khd->hqk', qpart, ksplit, preferred_element_type=jnp.floa...  55.3 us
    all_to_all x3, blocking collectives, copy_for_each(): lax.all_to_all(jnp.broadcast_to(x[None], (length, *x.shape)), axis, 0, 0,...  50.2 us
    all_to_all x1, waiting for transfers between devices, copy_for_each(): lax.all_to_all(jnp.broadcast_to(x[None], (length, *x.shape)), axis, 0, 0,...  24.1 us
    all_to_all x1, blocking collectives, sent_and_summed(): lax.all_to_all(tiles, axis, split_axis=0, concat_axis=0, tiled=True)  18.4 us
    all_to_all x1, waiting for transfers between devices, sent_and_summed(): lax.all_to_all(tiles, axis, split_axis=0, concat_axis=0, tiled=True)  13.9 us
    broadcast_in_dim x4, local copies, waits for them, and re-layouts, one_block(): jnp.repeat(jnp.repeat(mpart, BLOCK, axis=0), BLOCK, axis=1) > 0  13.9 us
  transfers between devices with their start and end apart: 4, of which 3 were waited for; matrix products, arithmetic and copies ran while one was open for 3% of the time, Pallas kernels for 0%

commit v1 on v0

v1 whole, which is shorter than its diff:
```python
import functools
import math

import jax
import jax.numpy as jnp
from jax import lax
from jax.experimental import pallas as pl
from jax.experimental.pallas import tpu as pltpu
from jax.sharding import PartitionSpec as P

MESH = pl.DeviceIdType.MESH
D = 512
HEADS = 8
FF = 1024
BLOCK = 128
LAYERS = 2
HD = D // HEADS
LOW = -1e30
SCALE = math.log2(math.e) / math.sqrt(HD)
SHORT = 44
LONG = 128


def lists_kernel(mask_ref, out_ref):
    r, c = lax.axis_index("row"), lax.axis_index("col")
    z, t = r // 2, (r % 2) * 16 + c
    f32 = jnp.float32
    mask = mask_ref[...].astype(f32)
    iota = lambda shape, d: lax.broadcasted_iota(jnp.int32, shape, d)
    one = lambda cond: jnp.where(cond, 1.0, 0.0).astype(f32)
    dims = lambda a, b: (((a,), (b,)), ((), ()))
    dot = lambda a, b, d: lax.dot_general(a, b, d, preferred_element_type=f32)
    query_sel = one(iota((8, 128), 1) == iota((8, 128), 0) * 32 + t)
    key_sel = one(iota((128, 32), 0) == iota((128, 32), 1) + z * 32)
    by_key = dot(mask, query_sel, dims(0, 1))
    sub = dot(key_sel, by_key, dims(0, 0))
    before = dot(one(iota((32, 32), 1) < iota((32, 32), 0)), sub, dims(1, 0))
    totals = jnp.sum(sub, axis=0, keepdims=True)
    lanes = iota((32, 128), 1).astype(f32)
    keys = iota((32, 128), 0).astype(f32)
    zero = jnp.zeros((1, 128), f32)
    q_row, k_row, f_row, e_row, start = zero, zero, zero, zero, jnp.zeros((1, 1), f32)
    lane = iota((1, 128), 1)
    for q in range(4):
        rank = before[:, q : q + 1] + start
        hit = jnp.where((rank == lanes) & (sub[:, q : q + 1] > 0.5), 1.0, 0.0)
        taken = jnp.sum(hit, axis=0, keepdims=True)
        q_row += taken * float(q)
        k_row += jnp.sum(hit * keys, axis=0, keepdims=True)
        f_row += jnp.where(lane.astype(f32) == start, taken, 0.0)
        total = totals[:, q : q + 1]
        last = jnp.where(total > 0.5, start + total, 0.0)
        e_row += jnp.where(lane == q, last, 0.0)
        start = start + total
    plane_t = one(iota((32, 128), 1) % 32 == iota((32, 128), 0))
    plane_z = one(iota((128, 8), 0) // 32 == iota((128, 8), 1))
    counts = dot(dot(plane_t, mask, dims(1, 0)), plane_z, dims(1, 0))
    most = jnp.max(jnp.max(counts, axis=1, keepdims=True), axis=0, keepdims=True)
    out_ref[0:1, :] = q_row.astype(jnp.int32)
    out_ref[1:2, :] = k_row.astype(jnp.int32)
    out_ref[2:3, :] = f_row.astype(jnp.int32)
    out_ref[3:4, :] = e_row.astype(jnp.int32)
    out_ref[4:8, :] = jnp.broadcast_to(most, (4, 128)).astype(jnp.int32)


def normed(values, gain, bias):
    center = values - jnp.mean(values, axis=-1, keepdims=True)
    spread = jnp.mean(center * center, axis=-1, keepdims=True)
    return center * lax.rsqrt(spread + 1e-05) * gain + bias


def layers_kernel(
    slots, meta, x_hbm, wqkv_hbm, wout_hbm, wup_hbm, wdown_hbm, gain, bias, out_ref,
    xg, xz, kbuf, vbuf, qbd, so, sm, osend, msend, orecv, mrecv, attn_t,
    wqkv, wout, wup, wdown, wq_t, wv_t,
    in_sem, w_sem, own_sem, mate_sem, z_sem, o_sem, m_sem, send_sem,
):
    f32, bf16 = jnp.float32, jnp.bfloat16
    r, c = lax.axis_index("row"), lax.axis_index("col")
    z, y, co = r // 2, c // 4, c % 2
    x = (r % 2) * 2 + (c // 2) % 2

    def device(px, py, pz, pc):
        return (pz * 2 + px // 2, py * 4 + (px % 2) * 2 + pc)

    def place(p, q):
        dx, dy = p * (1 - co) + q * co, q * (1 - co) + p * co
        return (x + dx + 8) % 4, (y + dy + 8) % 4

    def chip_of(p, q):
        px, py = place(p, q)
        return (px // 2) * 8 + py * 2 + px % 2

    def block_of(p, q):
        return chip_of(p, q) * 2 + co

    def peer(p, q):
        px, py = place(p, q)
        return device(px, py, z, co)

    def z_peer(d):
        return device(x, y, (z + d) % 4, co)

    mate = device(x, y, z, 1 - co)
    own = block_of(0, 0)

    first = [
        pltpu.make_async_copy(x_hbm, xg.at[0, own], in_sem.at[0]),
        pltpu.make_async_copy(x_hbm, xz.at[0, z], in_sem.at[1]),
    ]
    for cp in first:
        cp.start()

    def weight_copies(l):
        return [
            pltpu.make_async_copy(src.at[l], dst.at[l], w_sem.at[i, l])
            for i, (src, dst) in enumerate(
                ((wqkv_hbm, wqkv), (wout_hbm, wout), (wup_hbm, wup), (wdown_hbm, wdown))
            )
        ]

    for l in range(LAYERS):
        for cp in weight_copies(l):
            cp.start()

    barrier = pltpu.get_barrier_semaphore()
    others = [peer(1, 0), peer(-1, 0), peer(2, 0), peer(0, 1), peer(0, -1), peer(0, 2)]
    others += [z_peer(1), z_peer(2), z_peer(3), mate]
    for other in others:
        pl.semaphore_signal(barrier, inc=1, device_id=other, device_id_type=MESH)

    qbd[...] = jnp.zeros_like(qbd)
    so[0] = jnp.zeros_like(so[0])
    for row in range(4):
        sm[0, row : row + 1, :] = jnp.full((1, 256), LOW if row % 2 == 0 else 0.0, f32)
    pl.semaphore_wait(barrier, len(others))
    for cp in first:
        cp.wait()

    def layer(l, carry):
        sends = []

        def send(src, dst, sem, to):
            cp = pltpu.make_async_remote_copy(
                src_ref=src, dst_ref=dst, send_sem=send_sem.at[l, len(sends)], recv_sem=sem,
                device_id=to, device_id_type=MESH,
            )
            cp.start()
            sends.append(cp)

        def index(p, q):
            return (p % 4) * 4 + q % 4

        def pass_on(p, q, da, db):
            block = xg.at[l, block_of(p, q)]
            send(block, block, own_sem.at[l, index(p - da, q - db)], peer(da, db))

        def to_mate(p, q):
            block = xg.at[l, block_of(p, q)]
            send(block, block, mate_sem.at[l, index(p, q)], mate)

        def arrived(block, sem):
            pltpu.make_async_remote_copy(
                src_ref=block, dst_ref=block, send_sem=send_sem.at[l, 47], recv_sem=sem,
                device_id=mate, device_id_type=MESH,
            ).wait_recv()

        def got(p, q):
            arrived(xg.at[l, block_of(p, q)], own_sem.at[l, index(p, q)])

        def got_mate(p, q):
            arrived(xg.at[l, chip_of(p, q) * 2 + 1 - co], mate_sem.at[l, index(q, p)])

        pass_on(0, 0, 0, 1)
        pass_on(0, 0, 0, -1)
        pass_on(0, 0, 1, 0)
        pass_on(0, 0, -1, 0)
        pass_on(0, 0, 2, 0)
        to_mate(0, 0)
        for d in (1, 3, 2):
            send(xg.at[l, own], xz.at[l, z], z_sem.at[l, (-d) % 4], z_peer(d))

        weights = weight_copies(l)
        weights[0].wait()
        wq_t[...] = wqkv[l, :, 0:D].T
        wv_t[...] = wqkv[l, :, 2 * D : 3 * D].T

        def project(chip):
            rows = xg[l, pl.ds(chip * 2, 2)].reshape(2 * BLOCK, D)
            keys = jnp.dot(rows, wqkv[l, :, D : 2 * D], preferred_element_type=f32).astype(bf16)
            vals = lax.dot_general(
                wv_t[...], rows, (((1,), (1,)), ((), ())), preferred_element_type=f32
            ).astype(bf16)
            for i in range(2):
                for g in range(2):
                    kbuf[g, chip * 2 + i] = keys[i * BLOCK : (i + 1) * BLOCK, g * 256 : (g + 1) * 256]
                    vbuf[g, chip * 2 + i] = vals[g * 256 : (g + 1) * 256, i * BLOCK : (i + 1) * BLOCK]

        def project_all(places):
            def step(i, carry):
                p, q = places[0]
                for n, (pn, qn) in enumerate(places[1:], 1):
                    p, q = jnp.where(i == n, pn, p), jnp.where(i == n, qn, q)
                project(chip_of(p, q))
                return carry

            lax.fori_loop(0, len(places), step, 0)

        for p in (1, 3):
            got(p, 0)
            to_mate(p, 0)
            pass_on(p, 0, 0, 1)
            pass_on(p, 0, 0, -1)
        got(0, 3)
        pass_on(0, 3, 0, 1)
        to_mate(0, 3)
        got(0, 1)
        to_mate(0, 1)
        got(2, 0)
        pass_on(2, 0, 0, 1)
        pass_on(2, 0, 0, -1)
        to_mate(2, 0)
        got_mate(0, 0)
        near = [(1, 0), (3, 0), (0, 3), (0, 1)]
        for p, q in near:
            got_mate(p, q)
        project_all([(0, 0)] + near)

        for d in range(1, 4):
            arrived(xz.at[l, (z + d) % 4], z_sem.at[l, d])
        q_t = lax.dot_general(
            wq_t[...], xz[l].reshape(4 * BLOCK, D), (((1,), (1,)), ((), ())), preferred_element_type=f32
        ).astype(bf16)
        for b in range(4):
            for h in range(HEADS):
                qbd[b, h // 2, (h % 2) * HD : (h % 2 + 1) * HD, (h % 2) * BLOCK : (h % 2 + 1) * BLOCK] = q_t[
                    h * HD : (h + 1) * HD, b * BLOCK : (b + 1) * BLOCK
                ]

        got(0, 2)
        to_mate(0, 2)
        for p in (1, 3):
            got(p, 1)
            pass_on(p, 1, 0, -1)
            to_mate(p, 1)
            got(p, 3)
            to_mate(p, 3)
        got(2, 3)
        pass_on(2, 3, 0, 1)
        to_mate(2, 3)
        got(2, 1)
        to_mate(2, 1)
        diagonal = [(2, 0), (0, 2), (1, 1), (3, 1), (1, 3), (3, 3)]
        for p, q in diagonal:
            got_mate(p, q)
        project_all(diagonal)
        far = [(1, 2), (3, 2), (2, 2)]
        for p, q in far:
            got(p, q)
            to_mate(p, q)
        far = [(1, 2), (3, 2), (2, 1), (2, 3), (2, 2)]
        for p, q in far:
            got_mate(p, q)
        project_all(far)

        for g in range(2):

            def slot(s, carry):
                qi, kj = meta[0, s], meta[1, s]
                new = jnp.full((1, 256), meta[2, s], jnp.int32) > 0
                keys = kbuf[g, kj]
                vals = vbuf[g, kj]
                for pr in range(2):
                    scores = jnp.dot(
                        keys[:, pr * 128 : (pr + 1) * 128], qbd[qi, g * 2 + pr], preferred_element_type=f32
                    )
                    old = jnp.where(new, LOW, sm[s, 2 * pr : 2 * pr + 1, :])
                    top = jnp.maximum(old, jnp.max(scores, axis=0, keepdims=True))
                    keep = jnp.exp2((old - top) * SCALE)
                    p = jnp.exp2((scores - top) * SCALE)
                    mass = sm[s, 2 * pr + 1 : 2 * pr + 2, :] * keep + jnp.sum(p, axis=0, keepdims=True)
                    sm[s + 1, 2 * pr : 2 * pr + 1, :] = top
                    sm[s + 1, 2 * pr + 1 : 2 * pr + 2, :] = mass
                    pb = p.astype(bf16)
                    for hh in range(2):
                        at = (pr * 2 + hh) * HD
                        part = jnp.dot(
                            vals[at : at + HD, :], pb[:, hh * 128 : (hh + 1) * 128], preferred_element_type=f32
                        )
                        so[s + 1, at : at + HD, :] = (
                            so[s, at : at + HD, :] * keep[:, hh * 128 : (hh + 1) * 128] + part
                        )
                return carry

            lax.fori_loop(0, slots, slot, 0)
            for d in (2, 1, 3):
                pz = (z + d) % 4
                e = meta[3, pz]
                osend[l, g, d] = so[e].astype(bf16)
                msend[l, g, d] = sm[e]
                send(osend.at[l, g, d], orecv.at[l, g, z], o_sem.at[l, g, (-d) % 4], z_peer(d))
                send(msend.at[l, g, d], mrecv.at[l, g, z], m_sem.at[l, g, (-d) % 4], z_peer(d))
            e = meta[3, z]
            orecv[l, g, z] = so[e].astype(bf16)
            mrecv[l, g, z] = sm[e]

        for cp in weights[1:]:
            cp.wait()
        for g in range(2):
            for d in range(1, 4):
                pz = (z + d) % 4
                arrived(orecv.at[l, g, pz], o_sem.at[l, g, d])
                arrived(mrecv.at[l, g, pz], m_sem.at[l, g, d])
            for pr in range(2):
                tops = [mrecv[l, g, i, 2 * pr : 2 * pr + 1, :] for i in range(4)]
                top = jnp.maximum(jnp.maximum(tops[0], tops[1]), jnp.maximum(tops[2], tops[3]))
                shares = [jnp.exp2((tops[i] - top) * SCALE) for i in range(4)]
                mass = sum(shares[i] * mrecv[l, g, i, 2 * pr + 1 : 2 * pr + 2, :] for i in range(4))
                shares = [share / mass for share in shares]
                for hh in range(2):
                    at = (pr * 2 + hh) * HD
                    half = slice(hh * 128, (hh + 1) * 128)
                    attn_t[g * 256 + at : g * 256 + at + HD, :] = sum(
                        orecv[l, g, i, at : at + HD, :].astype(f32) * shares[i][:, half] for i in range(4)
                    ).astype(bf16)

        mixed = lax.dot_general(
            attn_t[...], wout[l], (((0,), (0,)), ((), ())), preferred_element_type=f32
        )
        hidden = normed(xg[l, own].astype(f32) + mixed, gain[l, 0:1, :], bias[l, 0:1, :]).astype(bf16)
        up = jax.nn.gelu(jnp.dot(hidden, wup[l], preferred_element_type=f32)).astype(bf16)
        down = jnp.dot(up, wdown[l], preferred_element_type=f32)
        result = normed(hidden.astype(f32) + down, gain[l, 1:2, :], bias[l, 1:2, :]).astype(bf16)

        @pl.when(l == 0)
        def _():
            xg[1, own] = result
            xz[1, z] = result

        @pl.when(l == 1)
        def _():
            out_ref[...] = result

        for cp in sends:
            cp.wait_send()
        return carry

    lax.fori_loop(0, LAYERS, layer, 0)


def run_layers(slots, collective_id, meta, *arrays):
    vmem, bf16, f32 = pltpu.VMEM, jnp.bfloat16, jnp.float32
    dma = pltpu.SemaphoreType.DMA
    anywhere = pl.BlockSpec(memory_space=pl.ANY)
    whole = pl.BlockSpec(memory_space=pltpu.VMEM)
    return pl.pallas_call(
        functools.partial(layers_kernel, slots),
        out_shape=jax.ShapeDtypeStruct((BLOCK, D), bf16),
        in_specs=[pl.BlockSpec(memory_space=pltpu.SMEM)] + [anywhere] * 5 + [whole] * 2,
        out_specs=whole,
        scratch_shapes=[
            vmem((2, 32, BLOCK, D), bf16),
            vmem((2, 4, BLOCK, D), bf16),
            vmem((2, 32, BLOCK, 256), bf16),
            vmem((2, 32, 256, BLOCK), bf16),
            vmem((4, 4, 128, 256), bf16),
            vmem((slots + 1, 256, 128), f32),
            vmem((slots + 1, 4, 256), f32),
            vmem((2, 2, 4, 256, 128), bf16),
            vmem((2, 2, 4, 4, 256), f32),
            vmem((2, 2, 4, 256, 128), bf16),
            vmem((2, 2, 4, 4, 256), f32),
            vmem((D, BLOCK), bf16),
            vmem((2, D, 3 * D), bf16),
            vmem((2, D, D), bf16),
            vmem((2, D, FF), bf16),
            vmem((2, FF, D), bf16),
            vmem((D, D), bf16),
            vmem((D, D), bf16),
            dma((2,)),
            dma((4, 2)),
            dma((2, 16)),
            dma((2, 16)),
            dma((2, 4)),
            dma((2, 2, 4)),
            dma((2, 2, 4)),
            dma((2, 48)),
        ],
        compiler_params=pltpu.CompilerParams(
            collective_id=collective_id, has_side_effects=True, vmem_limit_bytes=60 * 1024 * 1024
        ),
        name=f"layers_{slots}",
    )(meta, *arrays)


def per_device(node_feats, block_mask, w_qkv, w_out, w_up, w_down, ln_gain, ln_bias):
    meta = pl.pallas_call(
        lists_kernel,
        out_shape=jax.ShapeDtypeStruct((8, 128), jnp.int32),
        in_specs=[pl.BlockSpec(memory_space=pltpu.VMEM)],
        out_specs=pl.BlockSpec(memory_space=pltpu.VMEM),
        name="lists",
    )(block_mask)
    return lax.cond(
        meta[4, 0] <= SHORT,
        functools.partial(run_layers, SHORT, 0),
        functools.partial(run_layers, LONG, 1),
        meta, node_feats, w_qkv, w_out, w_up, w_down, ln_gain, ln_bias,
    )


def solution(mesh):
    placed = (P(("row", "col"), None), P(), P(), P(), P(), P(), P(), P())
    return jax.shard_map(
        per_device, mesh=mesh, in_specs=placed, out_specs=P(("row", "col"), None), check_vma=False
    )
```

time: 403 us -> 137 us (0.34)
  Pallas kernels: 0 us -> 135 us
  matrix products: 132 us -> 0 us
  blocking collectives: 68.6 us -> 0 us
  other arithmetic: 67.7 us -> 0 us
  local copies, waits for them, and re-layouts: 61.7 us -> 1.17 us
  waiting for transfers between devices: 43.6 us -> 0 us
  between operations: 13.9 us -> 0.67 us
  starting transfers between devices: 12.1 us -> 0 us
    pallas_call x0 -> x2, Pallas kernels: none -> 135 us  [the longest x1 133 us: run_layers(): pl.pallas_call(functools.partial(layers_kernel, slots), out_shape=jax.Sha...]
    dot_general x16 -> x0, matrix products: 132 us -> none  [the longest x4 62 us: one_block(): jnp.einsum('hqk,khd->qhd', weights.astype(jnp.bfloat16), vsplit, preferre...]
    all_to_all x4 -> x0, blocking collectives: 68.6 us -> none  [the longest x3 50.2 us: copy_for_each(): lax.all_to_all(jnp.broadcast_to(x[None], (length, *x.shape)), axis, 0, 0,...]
    reduce_sum x10 -> x0, other arithmetic: 61.7 us -> none  [the longest x4 60.7 us: one_block(): mass = jnp.sum(weights, axis=-1)]
    all_to_all x2 -> x0, waiting for transfers between devices: 38 us -> none  [the longest x1 24.1 us: copy_for_each(): lax.all_to_all(jnp.broadcast_to(x[None], (length, *x.shape)), axis, 0, 0,...]
    broadcast_in_dim x12 -> x0, local copies, waits for them, and re-layouts: 15.2 us -> none  [the longest x4 13.9 us: one_block(): jnp.repeat(jnp.repeat(mpart, BLOCK, axis=0), BLOCK, axis=1) > 0]
    all_to_all x2 -> x0, starting transfers between devices: 11.9 us -> none  [the longest x1 8.31 us: copy_for_each(): lax.all_to_all(jnp.broadcast_to(x[None], (length, *x.shape)), axis, 0, 0,...]
    dynamic_update_slice x12 -> x0, local copies, waits for them, and re-layouts: 10.5 us -> none  [partial_attention(): summed, peak, mass = lax.map(one_block, (qsplit, mask_rows))]
  transfers between devices with their start and end apart: 4 -> 0, of which waited for: 3 -> 0; matrix products, arithmetic and copies ran while one was open for 3% -> 0% of each run, Pallas kernels for 0% -> 0%
where the time goes in v1:
time: 137 us; the launch traced here: 136 us
  Pallas kernels  135 us (99%)
    pallas_call x1, Pallas kernels, run_layers(): pl.pallas_call(functools.partial(layers_kernel, slots), out_shape=jax.Sha...  133 us

profile of v1, /device:TPU:1, one launch (start us, length us, event | category | flops | bytes accessed | tf_op | source)
XLA Modules:
  0.0 136.5 jit_solution(11104574200306549509)
XLA Ops:
  0.0 1.4 %lists.1 = s32[8,128]{1,0:T(8,128)S(1)} custom-call(s32[128,128]{1,0:T(8,128)} %mask_ref.1), custom_call_target="tpu_custom_call" | custom-call | tf_op jit(solution)/shard_map/lists/pallas_call | solution.py:397
  1.4 0.5 slice.3
  2.6 133.2 %conditional.1 = (bf16[128,512]{1,0:T(8,128)(2,1)S(1)}) conditional(s32[]{:T(128)} %bitcast, (s32[8,128]{1,0:T(8,128)S(1)}, bf16[128,512]{1,0:T(8,128)(2,1)}, bf16[2,512,1536]{2,1,0:T(8,128)(2,1)}, bf16[2,512,512]{2,1,0:T(8,128)(2,1)}, bf16[2,512,1024]{2,1,0:T(8,128)(2,1)}, /*index=5*/bf16[2,1024,512]{2,1,0:T(8,128)(2,1)}, f32[2,2,512]{2,1,0:T(2,128)}, ...), branch_computations={%region_0.0_spmd, %region_1.0_spmd} | conditional | bytes 8 | solution.py:404
  2.6 133.2 %layers_44.1 = bf16[128,512]{1,0:T(8,128)(2,1)S(1)} custom-call(s32[8,128]{1,0:T(8,128)S(1)} %get-tuple-element.48.meta, bf16[128,512]{1,0:T(8,128)(2,1)} %get-tuple-element.49.x_hbm, bf16[2,512,1536]{2,1,0:T(8,128)(2,1)} %get-tuple-element.50.wqkv_hbm, bf16[2,512,512]{2,1,0:T(8,128)(2,1)} %get-tuple-element.51.wout_hbm, ...), custom_call_target="tpu_custom_call" | custom-call | tf_op jit(solution)/shard_map/cond/branch_1_fun/layers_44/pallas_call | solution.py:356
  135.8 0.7 copy.14

commit v2 on v1

--- a/solution.py
+++ b/solution.py
@@ -19,6 +19,7 @@
 SCALE = math.log2(math.e) / math.sqrt(HD)
 SHORT = 44
 LONG = 128
+STEP = {SHORT: 22, LONG: 8}
 
 
 def lists_kernel(mask_ref, out_ref):
@@ -265,7 +266,7 @@
 
         for g in range(2):
 
-            def slot(s, carry):
+            def slot(s):
                 qi, kj = meta[0, s], meta[1, s]
                 new = jnp.full((1, 256), meta[2, s], jnp.int32) > 0
                 keys = kbuf[g, kj]
@@ -290,9 +291,13 @@
                         so[s + 1, at : at + HD, :] = (
                             so[s, at : at + HD, :] * keep[:, hh * 128 : (hh + 1) * 128] + part
                         )
+
+            def steps(i, carry):
+                for n in range(STEP[slots]):
+                    slot(i * STEP[slots] + n)
                 return carry
 
-            lax.fori_loop(0, slots, slot, 0)
+            lax.fori_loop(0, slots // STEP[slots], steps, 0)
             for d in (2, 1, 3):
                 pz = (z + d) % 4
                 e = meta[3, pz]

time: 137 us -> 83.6 us (0.61)
  Pallas kernels: 135 us -> 81.4 us
    pallas_call x1, Pallas kernels: 133 us -> 79.9 us  [run_layers(): pl.pallas_call(functools.partial(layers_kernel, slots), out_shape=jax.Sha...]
where the time goes in v2:
time: 83.6 us; the launch traced here: 83.4 us
  Pallas kernels  81.4 us (97%)
  local copies, waits for them, and re-layouts  1.17 us (1%)
    pallas_call x1, Pallas kernels, run_layers(): pl.pallas_call(functools.partial(layers_kernel, slots), out_shape=jax.Sha...  79.9 us

profile of v2, /device:TPU:1, one launch (start us, length us, event | category | flops | bytes accessed | tf_op | source)
XLA Modules:
  0.0 83.4 jit_solution(8333065974087696666)
XLA Ops:
  0.0 1.4 %lists.1 = s32[8,128]{1,0:T(8,128)S(1)} custom-call(s32[128,128]{1,0:T(8,128)} %mask_ref.1), custom_call_target="tpu_custom_call" | custom-call | tf_op jit(solution)/shard_map/lists/pallas_call | solution.py:402
  1.4 0.5 slice.3
  2.6 80.1 %conditional.1 = (bf16[128,512]{1,0:T(8,128)(2,1)S(1)}) conditional(s32[]{:T(128)} %bitcast, (s32[8,128]{1,0:T(8,128)S(1)}, bf16[128,512]{1,0:T(8,128)(2,1)}, bf16[2,512,1536]{2,1,0:T(8,128)(2,1)}, bf16[2,512,512]{2,1,0:T(8,128)(2,1)}, bf16[2,512,1024]{2,1,0:T(8,128)(2,1)}, /*index=5*/bf16[2,1024,512]{2,1,0:T(8,128)(2,1)}, f32[2,2,512]{2,1,0:T(2,128)}, ...), branch_computations={%region_0.0_spmd, %region_1.0_spmd} | conditional | bytes 8 | solution.py:409
  2.8 79.9 %layers_44.1 = bf16[128,512]{1,0:T(8,128)(2,1)S(1)} custom-call(s32[8,128]{1,0:T(8,128)S(1)} %get-tuple-element.48.meta, bf16[128,512]{1,0:T(8,128)(2,1)} %get-tuple-element.49.x_hbm, bf16[2,512,1536]{2,1,0:T(8,128)(2,1)} %get-tuple-element.50.wqkv_hbm, bf16[2,512,512]{2,1,0:T(8,128)(2,1)} %get-tuple-element.51.wout_hbm, ...), custom_call_target="tpu_custom_call" | custom-call | tf_op jit(solution)/shard_map/cond/branch_1_fun/layers_44/pallas_call | solution.py:361
  82.7 0.7 copy.14

commit v3 on v1

v3 whole, which is shorter than its diff:
```python
import functools
import math

import jax
import jax.numpy as jnp
from jax import lax
from jax.experimental import pallas as pl
from jax.experimental.pallas import tpu as pltpu
from jax.sharding import PartitionSpec as P

MESH = pl.DeviceIdType.MESH
D = 512
HEADS = 8
FF = 1024
BLOCK = 128
LAYERS = 2
HD = D // HEADS
LOW = -1e30
SCALE = math.log2(math.e) / math.sqrt(HD)
H = 2
NSEND = 104
SHORT = (36, 36)
LONG = (112, 144)
STEP = {36: 36, 112: 16, 144: 16}
SLOTS = 256


def in_line(a, b):
    same_x = (a >> 3) * 2 + (a & 1) == (b >> 3) * 2 + (b & 1)
    return jnp.where(same_x | (((a >> 1) & 3) == ((b >> 1) & 3)), 1.0, 0.0)


def lists_kernel(mask_ref, out_ref, fits_ref):
    r, c = lax.axis_index("row"), lax.axis_index("col")
    z, chip = r // 2, (r % 2) * 8 + c // 2
    f32 = jnp.float32
    mask = mask_ref[...].astype(f32)
    iota = lambda shape, d: lax.broadcasted_iota(jnp.int32, shape, d)
    one = lambda cond: jnp.where(cond, 1.0, 0.0).astype(f32)
    dims = lambda a, b: (((a,), (b,)), ((), ()))
    dot = lambda a, b, d: lax.dot_general(a, b, d, preferred_element_type=f32)
    plane_chip = one(((iota((16, 128), 1) & 31) >> 1) == iota((16, 128), 0))
    plane_z = one((iota((128, 8), 0) >> 5) == iota((128, 8), 1))
    close = in_line(iota((16, 128), 0), (iota((16, 128), 1) & 31) >> 1)
    linked = dot(plane_chip, mask, dims(1, 0))
    near_most = jnp.max(dot(linked * close, plane_z, dims(1, 0)))
    far_most = jnp.max(dot(linked * (1.0 - close), plane_z, dims(1, 0)))
    fits = (near_most <= SHORT[0]) & (far_most <= SHORT[1])
    fits_ref[0, 0] = fits.astype(jnp.int32)

    b = iota((8, 128), 0)
    query_sel = one(iota((8, 128), 1) == (b >> 1) * 32 + chip * 2 + (b & 1))
    key_sel = one(iota((128, 32), 0) == iota((128, 32), 1) + z * 32)
    sub = dot(key_sel, dot(mask, query_sel, dims(0, 1)), dims(0, 0))
    near = in_line(iota((32, 8), 0) >> 1, chip)
    earlier = one(iota((32, 32), 1) < iota((32, 32), 0))
    lanes = iota((32, SLOTS), 1).astype(f32)
    keys = iota((32, SLOTS), 0).astype(f32)
    lane = iota((1, SLOTS), 1).astype(f32)
    zero = jnp.zeros((1, SLOTS), f32)
    rows, last = [], [jnp.zeros((1, 1), f32)] * 8
    for group in (sub * near, sub * (1.0 - near)):
        q_row = k_row = n_row = p_row = e_row = zero
        before = dot(earlier, group, dims(1, 0))
        totals = jnp.sum(group, axis=0, keepdims=True)
        start = jnp.zeros((1, 1), f32)
        for q in range(8):
            rank = before[:, q : q + 1] + start
            hit = jnp.where((rank == lanes) & (group[:, q : q + 1] > 0.5), 1.0, 0.0)
            taken = jnp.sum(hit, axis=0, keepdims=True)
            q_row += taken * float(q)
            k_row += jnp.sum(hit * keys, axis=0, keepdims=True)
            fresh = jnp.where(lane == start, taken, 0.0)
            n_row += fresh
            p_row += fresh * last[q]
            total = totals[:, q : q + 1]
            last[q] = jnp.where(total > 0.5, start + total, 0.0)
            e_row += jnp.where(lane == float(q), last[q], 0.0)
            start = start + total
        rows += [q_row, k_row, n_row, p_row, e_row]
    for n, row in enumerate(rows):
        out_ref[n : n + 1, :] = row.astype(jnp.int32)
    out_ref[10:16, :] = jnp.zeros((6, SLOTS), jnp.int32)


def normed(values, gain, bias):
    center = values - jnp.mean(values, axis=-1, keepdims=True)
    spread = jnp.mean(center * center, axis=-1, keepdims=True)
    return center * lax.rsqrt(spread + 1e-05) * gain + bias


def layers_kernel(
    counts, meta, x_hbm, wqkv_hbm, wout_hbm, wup_hbm, wdown_hbm, gain, bias, out_ref,
    xg, xz, kbuf, vbuf, qbd, so, sm, so_far, sm_far, osend, msend, orecv, mrecv, attn_t,
    wqkv, wout, wup, wdown, wq_t, wv_t,
    in_sem, w_sem, own_sem, mate_sem, z_sem, zm_sem, o_sem, m_sem, send_sem,
):
    f32, bf16 = jnp.float32, jnp.bfloat16
    r, c = lax.axis_index("row"), lax.axis_index("col")
    z, y, co = r // 2, c // 4, c % 2
    x = (r % 2) * 2 + (c // 2) % 2
    rows_of = BLOCK // H

    def device(px, py, pz, pc):
        return (pz * 2 + px // 2, py * 4 + (px % 2) * 2 + pc)

    def place(p, q):
        dx, dy = p * (1 - co) + q * co, q * (1 - co) + p * co
        return (x + dx + 8) % 4, (y + dy + 8) % 4

    def chip_of(p, q):
        px, py = place(p, q)
        return (px // 2) * 8 + py * 2 + px % 2

    def block_of(p, q):
        return chip_of(p, q) * 2 + co

    def peer(p, q):
        px, py = place(p, q)
        return device(px, py, z, co)

    def z_peer(d, core):
        return device(x, y, (z + d) % 4, core)

    mate = device(x, y, z, 1 - co)
    own = block_of(0, 0)

    first = [
        pltpu.make_async_copy(x_hbm, xg.at[0, own], in_sem.at[0]),
    ]
    for cp in first:
        cp.start()

    def weight_copies(l):
        return [
            pltpu.make_async_copy(src.at[l], dst.at[l], w_sem.at[i, l])
            for i, (src, dst) in enumerate(
                ((wqkv_hbm, wqkv), (wout_hbm, wout), (wup_hbm, wup), (wdown_hbm, wdown))
            )
        ]

    for l in range(LAYERS):
        for cp in weight_copies(l):
            cp.start()

    barrier = pltpu.get_barrier_semaphore()
    others = [peer(1, 0), peer(-1, 0), peer(2, 0), peer(0, 1), peer(0, -1), peer(0, 2)]
    others += [z_peer(d, core) for d in (1, 2, 3) for core in (0, 1)] + [mate]
    for other in others:
        pl.semaphore_signal(barrier, inc=1, device_id=other, device_id_type=MESH)

    qbd[...] = jnp.zeros_like(qbd)
    for sums, marks in ((so, sm), (so_far, sm_far)):
        for g in range(2):
            sums[g, 0] = jnp.zeros((128, 128), f32)
            marks[0, 2 * g : 2 * g + 1, :] = jnp.full((1, 256), LOW, f32)
            marks[0, 2 * g + 1 : 2 * g + 2, :] = jnp.zeros((1, 256), f32)
    pl.semaphore_wait(barrier, len(others))
    for cp in first:
        cp.wait()

    def layer(l, carry):
        sends = []

        def send(src, dst, sem, to):
            cp = pltpu.make_async_remote_copy(
                src_ref=src, dst_ref=dst, send_sem=send_sem.at[l, len(sends)], recv_sem=sem,
                device_id=to, device_id_type=MESH,
            )
            cp.start()
            sends.append(cp)

        def index(p, q):
            return (p % 4) * 4 + q % 4

        def piece(block, h):
            return xg.at[l, block, pl.ds(h * rows_of, rows_of)]

        def pass_on(p, q, da, db, h):
            block = piece(block_of(p, q), h)
            send(block, block, own_sem.at[l, index(p - da, q - db) * H + h], peer(da, db))

        def to_mate(p, q, h):
            block = piece(block_of(p, q), h)
            send(block, block, mate_sem.at[l, index(p, q) * H + h], mate)

        def arrived(block, sem):
            pltpu.make_async_remote_copy(
                src_ref=block, dst_ref=block, send_sem=send_sem.at[l, NSEND - 1], recv_sem=sem,
                device_id=mate, device_id_type=MESH,
            ).wait_recv()

        def got(p, q, h):
            arrived(piece(block_of(p, q), h), own_sem.at[l, index(p, q) * H + h])

        def got_mate(p, q):
            for h in range(H):
                arrived(piece(chip_of(p, q) * 2 + 1 - co, h), mate_sem.at[l, index(q, p) * H + h])

        for h in range(H):
            pass_on(0, 0, 1, 0, h)
            pass_on(0, 0, -1, 0, h)
            pass_on(0, 0, 0, 1, h)
            pass_on(0, 0, 0, -1, h)
        for h in range(H):
            pass_on(0, 0, 2, 0, h)
            pass_on(0, 0, 0, 2, h)
        for h in range(H):
            to_mate(0, 0, h)
        for d in (1, 3, 2):
            send(xg.at[l, own], xz.at[l, z * 2 + co], z_sem.at[l, (-d) % 4], z_peer(d, co))

        weights = weight_copies(l)
        weights[0].wait()
        wq_t[...] = wqkv[l, :, pl.ds(pl.multiple_of(co * 256, 256), 256)].T
        wv_t[...] = wqkv[l, :, pl.ds(pl.multiple_of(2 * D + co * 256, 256), 256)].T

        def transposed_product(weight, rows):
            return lax.dot_general(weight, rows, (((1,), (1,)), ((), ())), preferred_element_type=f32).astype(bf16)

        def project(chip):
            rows = xg[l, pl.ds(chip * 2, 2)].reshape(2 * BLOCK, D)
            keys = jnp.dot(
                rows, wqkv[l, :, pl.ds(pl.multiple_of(D + co * 256, 256), 256)], preferred_element_type=f32
            ).astype(bf16)
            vals = transposed_product(wv_t[...], rows)
            for i in range(2):
                for g in range(2):
                    kbuf[g, chip * 2 + i] = keys[i * BLOCK : (i + 1) * BLOCK, g * 128 : (g + 1) * 128]
                    vbuf[g, chip * 2 + i] = vals[g * 128 : (g + 1) * 128, i * BLOCK : (i + 1) * BLOCK]

        def project_all(places):
            for p, q in places:
                project(chip_of(p, q))

        def queries(pz, rows):
            q_t = transposed_product(wq_t[...], rows.reshape(2 * BLOCK, D))
            for core in range(2):
                for h in range(4):
                    hh = h % 2
                    qbd[pz * 2 + core, h // 2, hh * HD : (hh + 1) * HD, hh * BLOCK : (hh + 1) * BLOCK] = q_t[
                        h * HD : (h + 1) * HD, core * BLOCK : (core + 1) * BLOCK
                    ]

        for h in range(H):
            for p in (1, 3):
                got(p, 0, h)
                pass_on(p, 0, 0, 1, h)
                pass_on(p, 0, 0, -1, h)
                to_mate(p, 0, h)
        for h in range(H):
            got(2, 0, h)
            pass_on(2, 0, 0, 1, h)
            pass_on(2, 0, 0, -1, h)
            pass_on(2, 0, 0, 2, h)
            to_mate(2, 0, h)
        for h in range(H):
            for q in (1, 3):
                got(0, q, h)
                to_mate(0, q, h)
        got_mate(0, 0)
        near = [(1, 0), (3, 0), (0, 3), (0, 1)]
        for p, q in near:
            got_mate(p, q)
        project_all([(0, 0)] + near)

        for d in range(1, 4):
            block = xz.at[l, ((z + d) % 4) * 2 + co]
            arrived(block, z_sem.at[l, d])
            send(block, block, zm_sem.at[l, d], mate)
        queries(z, xg[l, pl.ds(chip_of(0, 0) * 2, 2)])
        for h in range(H):
            for p in (1, 3):
                got(p, 1, h)
                pass_on(p, 1, 0, -1, h)
                to_mate(p, 1, h)
        for h in range(H):
            got(0, 2, h)
            to_mate(0, 2, h)
        for d in range(1, 4):
            pz = (z + d) % 4
            arrived(xz.at[l, pz * 2 + 1 - co], zm_sem.at[l, d])
            queries(pz, xz[l, pl.ds(pz * 2, 2)])
        middle = [(2, 0), (0, 2)]
        for p, q in middle:
            got_mate(p, q)
        project_all(middle)

        def attend(g, far):
            sums, marks = (so_far, sm_far) if far else (so, sm)
            row, count = (5, counts[1]) if far else (0, counts[0])

            def slot(s, top_before, mass_before):
                vals = vbuf[g, meta[row + 1, s]]
                scores = jnp.dot(
                    kbuf[g, meta[row + 1, s]], qbd[meta[row, s], g], preferred_element_type=f32
                )
                new = jnp.full((1, 256), meta[row + 2, s], jnp.int32) > 0
                if far:
                    start = meta[row + 3, s]
                    top_before = jnp.where(new, sm[start, 2 * g : 2 * g + 1, :], top_before)
                    mass_before = jnp.where(new, sm[start, 2 * g + 1 : 2 * g + 2, :], mass_before)
                else:
                    top_before = jnp.where(new, LOW, top_before)
                top = jnp.maximum(top_before, jnp.max(scores, axis=0, keepdims=True))
                keep = jnp.exp2((top_before - top) * SCALE)
                p = jnp.exp2((scores - top) * SCALE)
                mass = mass_before * keep + jnp.sum(p, axis=0, keepdims=True)
                marks[s + 1, 2 * g : 2 * g + 1, :] = top
                marks[s + 1, 2 * g + 1 : 2 * g + 2, :] = mass
                pb = p.astype(bf16)
                for hh in range(2):
                    at, half = slice(hh * HD, (hh + 1) * HD), slice(hh * 128, (hh + 1) * 128)
                    part = jnp.dot(vals[at, :], pb[:, half], preferred_element_type=f32)
                    before = sums[g, s, at, :]
                    if far:
                        before = jnp.where(new[:, :128], so[g, start, at, :], before)
                    sums[g, s + 1, at, :] = before * keep[:, half] + part
                return top, mass

            def steps(i, carry):
                for n in range(STEP[count]):
                    carry = slot(i * STEP[count] + n, *carry)
                return carry

            init = (jnp.full((1, 256), LOW, f32), jnp.zeros((1, 256), f32))
            lax.fori_loop(0, count // STEP[count], steps, init)

        def state(g, b):
            near, far = meta[4, b], meta[9, b]
            take = jnp.full((1, 128), far, jnp.int32) > 0
            sums = jnp.where(take, so_far[g, far], so[g, near])
            take = jnp.full((1, 256), far, jnp.int32) > 0
            marks = jnp.where(take, sm_far[far, 2 * g : 2 * g + 2, :], sm[near, 2 * g : 2 * g + 2, :])
            return sums.astype(bf16), marks

        for g in range(2):
            attend(g, False)

        for p, q in ((1, 3), (3, 3), (2, 1), (2, 3), (1, 2), (3, 2), (2, 2)):
            for h in range(H):
                got(p, q, h)
                to_mate(p, q, h)
        far = [(1, 1), (3, 1), (1, 3), (3, 3), (1, 2), (3, 2), (2, 1), (2, 3), (2, 2)]
        for p, q in far[:4]:
            got_mate(p, q)
        project_all(far[:4])
        for p, q in far[4:]:
            got_mate(p, q)
        project_all(far[4:])

        for g in range(2):
            attend(g, True)
            for n, (d, core) in enumerate([(d, core) for d in (2, 1, 3) for core in (0, 1)] + [(0, 1 - co)]):
                osend[l, g, n], msend[l, g, n] = state(g, ((z + d) % 4) * 2 + core)
                to, at = z_peer(d, core), z * 2 + co
                sem = ((-d) % 4) * 2 + co
                send(osend.at[l, g, n], orecv.at[l, g, at], o_sem.at[l, g, sem], to)
                send(msend.at[l, g, n], mrecv.at[l, g, at], m_sem.at[l, g, sem], to)
            orecv[l, g, z * 2 + co], mrecv[l, g, z * 2 + co] = state(g, z * 2 + co)

        for cp in weights[1:]:
            cp.wait()
        for g in range(2):
            for d, core in [(0, 1 - co)] + [(d, core) for d in (1, 3, 2) for core in (0, 1)]:
                at = ((z + d) % 4) * 2 + core
                arrived(orecv.at[l, g, at], o_sem.at[l, g, d * 2 + core])
                arrived(mrecv.at[l, g, at], m_sem.at[l, g, d * 2 + core])
            for core in range(2):
                tops = [mrecv[l, g, i * 2 + core, 0:1, :] for i in range(4)]
                top = jnp.maximum(jnp.maximum(tops[0], tops[1]), jnp.maximum(tops[2], tops[3]))
                shares = [jnp.exp2((tops[i] - top) * SCALE) for i in range(4)]
                mass = sum(shares[i] * mrecv[l, g, i * 2 + core, 1:2, :] for i in range(4))
                shares = [share / mass for share in shares]
                for hh in range(2):
                    at, half = slice(hh * HD, (hh + 1) * HD), slice(hh * 128, (hh + 1) * 128)
                    to = core * 256 + g * 128 + hh * HD
                    attn_t[to : to + HD, :] = sum(
                        orecv[l, g, i * 2 + core, at, :].astype(f32) * shares[i][:, half] for i in range(4)
                    ).astype(bf16)

        mixed = lax.dot_general(
            attn_t[...], wout[l], (((0,), (0,)), ((), ())), preferred_element_type=f32
        )
        hidden = normed(xg[l, own].astype(f32) + mixed, gain[l, 0:1, :], bias[l, 0:1, :]).astype(bf16)
        up = jax.nn.gelu(jnp.dot(hidden, wup[l], preferred_element_type=f32)).astype(bf16)
        down = jnp.dot(up, wdown[l], preferred_element_type=f32)
        result = normed(hidden.astype(f32) + down, gain[l, 1:2, :], bias[l, 1:2, :]).astype(bf16)

        @pl.when(l == 0)
        def _():
            xg[1, own] = result

        @pl.when(l == 1)
        def _():
            out_ref[...] = result

        assert len(sends) < NSEND
        for cp in sends:
            cp.wait_send()
        return carry

    lax.fori_loop(0, LAYERS, layer, 0)


def run_layers(counts, collective_id, meta, *arrays):
    vmem, bf16, f32 = pltpu.VMEM, jnp.bfloat16, jnp.float32
    dma = pltpu.SemaphoreType.DMA
    anywhere = pl.BlockSpec(memory_space=pl.ANY)
    whole = pl.BlockSpec(memory_space=pltpu.VMEM)
    near, far = counts[0] + 1, counts[1] + 1
    return pl.pallas_call(
        functools.partial(layers_kernel, counts),
        out_shape=jax.ShapeDtypeStruct((BLOCK, D), bf16),
        in_specs=[pl.BlockSpec(memory_space=pltpu.SMEM)] + [anywhere] * 5 + [whole] * 2,
        out_specs=whole,
        scratch_shapes=[
            vmem((2, 32, BLOCK, D), bf16),
            vmem((2, 8, BLOCK, D), bf16),
            vmem((2, 32, BLOCK, 128), bf16),
            vmem((2, 32, 128, BLOCK), bf16),
            vmem((8, 2, 128, 256), bf16),
            vmem((2, near, 128, 128), f32),
            vmem((near, 4, 256), f32),
            vmem((2, far, 128, 128), f32),
            vmem((far, 4, 256), f32),
            vmem((2, 2, 7, 128, 128), bf16),
            vmem((2, 2, 7, 2, 256), f32),
            vmem((2, 2, 8, 128, 128), bf16),
            vmem((2, 2, 8, 2, 256), f32),
            vmem((D, BLOCK), bf16),
            vmem((2, D, 3 * D), bf16),
            vmem((2, D, D), bf16),
            vmem((2, D, FF), bf16),
            vmem((2, FF, D), bf16),
            vmem((256, D), bf16),
            vmem((256, D), bf16),
            dma((1,)),
            dma((4, 2)),
            dma((2, 16 * H)),
            dma((2, 16 * H)),
            dma((2, 4)),
            dma((2, 4)),
            dma((2, 2, 8)),
            dma((2, 2, 8)),
            dma((2, NSEND)),
        ],
        compiler_params=pltpu.CompilerParams(
            collective_id=collective_id, has_side_effects=True, vmem_limit_bytes=67043328
        ),
        name=f"layers_{near}",
    )(meta, *arrays)


def per_device(node_feats, block_mask, w_qkv, w_out, w_up, w_down, ln_gain, ln_bias):
    meta, fits = pl.pallas_call(
        lists_kernel,
        out_shape=(jax.ShapeDtypeStruct((16, SLOTS), jnp.int32), jax.ShapeDtypeStruct((1, 1), jnp.int32)),
        in_specs=[pl.BlockSpec(memory_space=pltpu.VMEM)],
        out_specs=(pl.BlockSpec(memory_space=pltpu.VMEM), pl.BlockSpec(memory_space=pltpu.SMEM)),
        name="lists",
    )(block_mask)
    return lax.cond(
        fits[0, 0] > 0,
        functools.partial(run_layers, SHORT, 0),
        functools.partial(run_layers, LONG, 1),
        meta, node_feats, w_qkv, w_out, w_up, w_down, ln_gain, ln_bias,
    )


def solution(mesh):
    placed = (P(("row", "col"), None), P(), P(), P(), P(), P(), P(), P())
    return jax.shard_map(
        per_device, mesh=mesh, in_specs=placed, out_specs=P(("row", "col"), None), check_vma=False
    )
```

time: 137 us -> 79.4 us (0.58)
  Pallas kernels: 135 us -> 76.7 us
    pallas_call x2, Pallas kernels: 135 us -> 76.7 us  [the longest x1 74.4 us: run_layers(): pl.pallas_call(functools.partial(layers_kernel, counts), out_shape=jax.Sh...]
where the time goes in v3:
time: 79.4 us; the launch traced here: 79.1 us
  Pallas kernels  76.7 us (97%)
  local copies, waits for them, and re-layouts  1.57 us (2%)
    pallas_call x1, Pallas kernels, run_layers(): pl.pallas_call(functools.partial(layers_kernel, counts), out_shape=jax.Sh...  74.4 us
    pallas_call x1, Pallas kernels, per_device(): pl.pallas_call(lists_kernel, out_shape=(jax.ShapeDtypeStruct((16, SLOTS),...  2.3 us

profile of v3, /device:TPU:1, one launch (start us, length us, event | category | flops | bytes accessed | tf_op | source)
XLA Modules:
  0.0 79.1 jit_solution(11391913178985972809)
XLA Ops:
  0.0 2.3 %lists.1 = (s32[16,256]{1,0:T(8,128)}, s32[1,1]{1,0:T(1,128)}) custom-call(s32[128,128]{1,0:T(8,128)} %mask_ref.1), custom_call_target="tpu_custom_call" | custom-call | tf_op jit(solution)/shard_map/lists/pallas_call | solution.py:456
  2.9 74.6 %conditional.1 = (bf16[128,512]{1,0:T(8,128)(2,1)}) conditional(s32[]{:T(128)} %bitcast, (s32[16,256]{1,0:T(8,128)}, bf16[128,512]{1,0:T(8,128)(2,1)}, bf16[2,512,1536]{2,1,0:T(8,128)(2,1)}, bf16[2,512,512]{2,1,0:T(8,128)(2,1)}, bf16[2,512,1024]{2,1,0:T(8,128)(2,1)}, /*index=5*/bf16[2,1024,512]{2,1,0:T(8,128)(2,1)}, f32[2,2,512]{2,1,0:T(2,128)}, ...), branch_computations={%region_0.0_spmd, %region_1.0_spmd} | conditional | bytes 8 | solution.py:463
  3.0 74.4 %layers_37.1 = bf16[128,512]{1,0:T(8,128)(2,1)} custom-call(s32[16,256]{1,0:T(8,128)} %get-tuple-element.48.meta, bf16[128,512]{1,0:T(8,128)(2,1)} %get-tuple-element.49.x_hbm, bf16[2,512,1536]{2,1,0:T(8,128)(2,1)} %get-tuple-element.50.wqkv_hbm, bf16[2,512,512]{2,1,0:T(8,128)(2,1)} %get-tuple-element.51.wout_hbm, ...), custom_call_target="tpu_custom_call" | custom-call | tf_op jit(solution)/shard_map/cond/branch_1_fun/layers_37/pallas_call | solution.py:412
  77.6 1.6 %copy.14 = bf16[128,512]{1,0:T(8,128)(2,1)} copy(bf16[128,512]{1,0:T(8,128)(2,1)} %get-tuple-element.60) | data formatting | bytes 262144

commit v4 on v3

--- a/solution.py
+++ b/solution.py
@@ -17,7 +17,7 @@
 HD = D // HEADS
 LOW = -1e30
 SCALE = math.log2(math.e) / math.sqrt(HD)
-H = 2
+H = 1
 NSEND = 104
 SHORT = (36, 36)
 LONG = (112, 144)
@@ -58,26 +58,24 @@
     keys = iota((32, SLOTS), 0).astype(f32)
     lane = iota((1, SLOTS), 1).astype(f32)
     zero = jnp.zeros((1, SLOTS), f32)
-    rows, last = [], [jnp.zeros((1, 1), f32)] * 8
+    over_before = one(iota((8, 8), 0) < iota((8, 8), 1))
+    spread = one(iota((8, SLOTS), 0) == iota((8, SLOTS), 1))
+    rows, last = [], jnp.zeros((8, 8), f32)
     for group in (sub * near, sub * (1.0 - near)):
-        q_row = k_row = n_row = p_row = e_row = zero
-        before = dot(earlier, group, dims(1, 0))
-        totals = jnp.sum(group, axis=0, keepdims=True)
-        start = jnp.zeros((1, 1), f32)
+        q_row = k_row = n_row = p_row = zero
+        totals = jnp.broadcast_to(jnp.sum(group, axis=0, keepdims=True), (8, 8))
+        starts = dot(totals, over_before, dims(1, 0))
+        ranks = dot(earlier, group, dims(1, 0)) + starts[0:1, :]
         for q in range(8):
-            rank = before[:, q : q + 1] + start
-            hit = jnp.where((rank == lanes) & (group[:, q : q + 1] > 0.5), 1.0, 0.0)
+            hit = jnp.where((ranks[:, q : q + 1] == lanes) & (group[:, q : q + 1] > 0.5), 1.0, 0.0)
             taken = jnp.sum(hit, axis=0, keepdims=True)
             q_row += taken * float(q)
             k_row += jnp.sum(hit * keys, axis=0, keepdims=True)
-            fresh = jnp.where(lane == start, taken, 0.0)
+            fresh = jnp.where(lane == starts[0:1, q : q + 1], taken, 0.0)
             n_row += fresh
-            p_row += fresh * last[q]
-            total = totals[:, q : q + 1]
-            last[q] = jnp.where(total > 0.5, start + total, 0.0)
-            e_row += jnp.where(lane == float(q), last[q], 0.0)
-            start = start + total
-        rows += [q_row, k_row, n_row, p_row, e_row]
+            p_row += fresh * last[0:1, q : q + 1]
+        last = jnp.where(totals > 0.5, starts + totals, 0.0)
+        rows += [q_row, k_row, n_row, p_row, dot(last, spread, dims(1, 0))[0:1, :]]
     for n, row in enumerate(rows):
         out_ref[n : n + 1, :] = row.astype(jnp.int32)
     out_ref[10:16, :] = jnp.zeros((6, SLOTS), jnp.int32)
@@ -446,7 +444,7 @@
             dma((2, NSEND)),
         ],
         compiler_params=pltpu.CompilerParams(
-            collective_id=collective_id, has_side_effects=True, vmem_limit_bytes=67043328
+            collective_id=collective_id, has_side_effects=True, vmem_limit_bytes=(48 if counts == SHORT else 62) * 1024 * 1024
         ),
         name=f"layers_{near}",
     )(meta, *arrays)

time: 79.4 us -> 76.2 us (0.960)
  Pallas kernels: 76.7 us -> 74.5 us
  local copies, waits for them, and re-layouts: 1.57 us -> 0.66 us
    pallas_call x1, Pallas kernels: 74.4 us -> 72.8 us  [run_layers(): pl.pallas_call(functools.partial(layers_kernel, counts), out_shape=jax.Sh...]
    unnamed x1, local copies, waits for them, and re-layouts: 1.57 us -> 0.66 us
where the time goes in v4:
time: 76.2 us; the launch traced here: 76 us
  Pallas kernels  74.5 us (98%)
    pallas_call x1, Pallas kernels, run_layers(): pl.pallas_call(functools.partial(layers_kernel, counts), out_shape=jax.Sh...  72.8 us
    pallas_call x1, Pallas kernels, per_device(): pl.pallas_call(lists_kernel, out_shape=(jax.ShapeDtypeStruct((16, SLOTS),...  1.72 us

profile of v4, /device:TPU:1, one launch (start us, length us, event | category | flops | bytes accessed | tf_op | source)
XLA Modules:
  0.0 76.0 jit_solution(18369864370910715566)
XLA Ops:
  0.0 1.7 %lists.1 = (s32[16,256]{1,0:T(8,128)S(1)}, s32[1,1]{1,0:T(1,128)}) custom-call(s32[128,128]{1,0:T(8,128)} %mask_ref.1), custom_call_target="tpu_custom_call" | custom-call | tf_op jit(solution)/shard_map/lists/pallas_call | solution.py:454
  2.4 73.0 %conditional.1 = (bf16[128,512]{1,0:T(8,128)(2,1)S(1)}) conditional(s32[]{:T(128)} %bitcast, (s32[16,256]{1,0:T(8,128)S(1)}, bf16[128,512]{1,0:T(8,128)(2,1)}, bf16[2,512,1536]{2,1,0:T(8,128)(2,1)}, bf16[2,512,512]{2,1,0:T(8,128)(2,1)}, bf16[2,512,1024]{2,1,0:T(8,128)(2,1)}, /*index=5*/bf16[2,1024,512]{2,1,0:T(8,128)(2,1)}, f32[2,2,512]{2,1,0:T(2,128)}, ...), branch_computations={%region_0.0_spmd, %region_1.0_spmd} | conditional | bytes 8 | solution.py:461
  2.6 72.8 %layers_37.1 = bf16[128,512]{1,0:T(8,128)(2,1)S(1)} custom-call(s32[16,256]{1,0:T(8,128)S(1)} %get-tuple-element.48.meta, bf16[128,512]{1,0:T(8,128)(2,1)} %get-tuple-element.49.x_hbm, bf16[2,512,1536]{2,1,0:T(8,128)(2,1)} %get-tuple-element.50.wqkv_hbm, bf16[2,512,512]{2,1,0:T(8,128)(2,1)} %get-tuple-element.51.wout_hbm, ...), custom_call_target="tpu_custom_call" | custom-call | tf_op jit(solution)/shard_map/cond/branch_1_fun/layers_37/pallas_call | solution.py:410
  75.4 0.7 copy.14

commit v5 on v4

--- a/solution.py
+++ b/solution.py
@@ -335,7 +335,7 @@
         for g in range(2):
             attend(g, False)
 
-        for p, q in ((1, 3), (3, 3), (2, 1), (2, 3), (1, 2), (3, 2), (2, 2)):
+        for p, q in ((1, 3), (3, 3), (2, 1), (2, 3)):
             for h in range(H):
                 got(p, q, h)
                 to_mate(p, q, h)
@@ -343,6 +343,10 @@
         for p, q in far[:4]:
             got_mate(p, q)
         project_all(far[:4])
+        for p, q in ((1, 2), (3, 2), (2, 2)):
+            for h in range(H):
+                got(p, q, h)
+                to_mate(p, q, h)
         for p, q in far[4:]:
             got_mate(p, q)
         project_all(far[4:])

time: 76.2 us -> 78.4 us (1.029)
  Pallas kernels: 74.5 us -> 76.8 us
    pallas_call x1, Pallas kernels: 72.8 us -> 75 us  [run_layers(): pl.pallas_call(functools.partial(layers_kernel, counts), out_shape=jax.Sh...]
where the time goes in v5:
time: 78.4 us; the launch traced here: 78.3 us
  Pallas kernels  76.8 us (98%)
    pallas_call x1, Pallas kernels, run_layers(): pl.pallas_call(functools.partial(layers_kernel, counts), out_shape=jax.Sh...  75 us
    pallas_call x1, Pallas kernels, per_device(): pl.pallas_call(lists_kernel, out_shape=(jax.ShapeDtypeStruct((16, SLOTS),...  1.72 us

profile of v5, /device:TPU:1, one launch (start us, length us, event | category | flops | bytes accessed | tf_op | source)
XLA Modules:
  0.0 78.3 jit_solution(15019819961273444838)
XLA Ops:
  0.0 1.7 %lists.1 = (s32[16,256]{1,0:T(8,128)S(1)}, s32[1,1]{1,0:T(1,128)}) custom-call(s32[128,128]{1,0:T(8,128)} %mask_ref.1), custom_call_target="tpu_custom_call" | custom-call | tf_op jit(solution)/shard_map/lists/pallas_call | solution.py:458
  2.4 75.2 %conditional.1 = (bf16[128,512]{1,0:T(8,128)(2,1)S(1)}) conditional(s32[]{:T(128)} %bitcast, (s32[16,256]{1,0:T(8,128)S(1)}, bf16[128,512]{1,0:T(8,128)(2,1)}, bf16[2,512,1536]{2,1,0:T(8,128)(2,1)}, bf16[2,512,512]{2,1,0:T(8,128)(2,1)}, bf16[2,512,1024]{2,1,0:T(8,128)(2,1)}, /*index=5*/bf16[2,1024,512]{2,1,0:T(8,128)(2,1)}, f32[2,2,512]{2,1,0:T(2,128)}, ...), branch_computations={%region_0.0_spmd, %region_1.0_spmd} | conditional | bytes 8 | solution.py:465
  2.6 75.0 %layers_37.1 = bf16[128,512]{1,0:T(8,128)(2,1)S(1)} custom-call(s32[16,256]{1,0:T(8,128)S(1)} %get-tuple-element.48.meta, bf16[128,512]{1,0:T(8,128)(2,1)} %get-tuple-element.49.x_hbm, bf16[2,512,1536]{2,1,0:T(8,128)(2,1)} %get-tuple-element.50.wqkv_hbm, bf16[2,512,512]{2,1,0:T(8,128)(2,1)} %get-tuple-element.51.wout_hbm, ...), custom_call_target="tpu_custom_call" | custom-call | tf_op jit(solution)/shard_map/cond/branch_1_fun/layers_37/pallas_call | solution.py:414
  77.6 0.7 copy.14
